TPU v7x, 128 devices: a whole 4x4x4 slice. The times are simulated.
128 devices in a mesh: fit: 1, comp: 2 (over core), pts: 64 (over z, y, x).
Axes of the slice: x: 4, y: 4, z: 4, core: 2. Of those that a mesh axis runs over, the one named last changes fastest.
Arguments:
- points: bfloat16 [262144, 512], P(('fit', 'pts'))
- means_init: float32 [4096, 512], P(('fit', 'comp'))
- logw_init: float32 [4096], P(('fit', 'comp'))
- inv_temp: float32 [3], replicated
Outputs:
- output 1: float32 [4096, 512], P(('fit', 'comp'))
- output 2: float32 [4096], P(('fit', 'comp'))
- output 3: float32 [262144], P(('fit', 'pts'))
All inputs are finite; a program needn't handle non-finite values.
Results may differ from a plain program's by a relative error of at most 0.001.
Values are sent between devices in bfloat16 or wider.
A program may use at most 1 GiB of HBM per device.

v0:
```python
import jax
import jax.numpy as jnp
from jax import lax
from jax.sharding import PartitionSpec as P

PRIOR_ALPHA = 1e-3
COUNT_EPS = 1e-6


def solution(mesh):
    row_groups = mesh.shape["pts"]
    comp_groups = mesh.shape["comp"]

    def per_device(points, mean_vecs, log_w, inv_temp):
        n_total = points.shape[0] * row_groups
        k_total = mean_vecs.shape[0] * comp_groups
        x_sq = jnp.einsum("nd,nd->n", points, points, preferred_element_type=jnp.float32)
        log_norm = None
        for sweep_idx in range(inv_temp.shape[0]):
            mean_bf = mean_vecs.astype(jnp.bfloat16)
            mean_sq = jnp.sum(mean_vecs * mean_vecs, axis=1)
            cross_dot = jnp.einsum("nd,kd->nk", points, mean_bf, preferred_element_type=jnp.float32)
            logits = log_w[None, :] - inv_temp[sweep_idx] * (x_sq[:, None] - 2.0 * cross_dot + mean_sq[None, :])
            row_top = lax.pmax(jnp.max(logits, axis=1), "comp")
            exp_total = lax.psum(jnp.sum(jnp.exp(logits - row_top[:, None]), axis=1), "comp")
            log_norm = row_top + jnp.log(exp_total)
            resp_prob = jnp.exp(logits - log_norm[:, None])
            counts = jnp.sum(resp_prob, axis=0)
            stat_sums = jnp.einsum("nk,nd->kd", resp_prob.astype(jnp.bfloat16), points, preferred_element_type=jnp.float32)
            counts, stat_sums = lax.psum((counts, stat_sums), "pts")
            mean_vecs = stat_sums / (counts[:, None] + COUNT_EPS)
            log_w = jnp.log((counts + PRIOR_ALPHA) / (n_total + k_total * PRIOR_ALPHA))
        return mean_vecs, log_w, log_norm

    row_spec = P(("fit", "pts"))
    comp_spec = P(("fit", "comp"))
    return jax.shard_map(
        per_device,
        mesh=mesh,
        in_specs=(P(("fit", "pts"), None), P(("fit", "comp"), None), comp_spec, P()),
        out_specs=(P(("fit", "comp"), None), comp_spec, row_spec),
        check_vma=False,
    )
```

profile of v0, /device:TPU:0, one launch (start us, length us, event | category | flops | bytes accessed | tf_op | source)
XLA Modules:
  0.0 777.4 jit_solution(8621862990857108800)
XLA Ops:
  7.2 0.0 all-reduce.4.cloned.1.call-start
  7.2 1.4 fusion.19
  8.6 2.5 multiply_reduce_fusion.2
  11.1 3.1 fusion.15
  14.2 19.2 %fusion.20 = (f32[4096]{0:T(1024)S(1)}, f32[4096,2048]{0,1:T(8,128)}) fusion(f32[2048]{0:T(1024)S(1)} %multiply_reduce_fusion.2, bf16[4096,512]{1,0:T(8,128)(2,1)} %param.4, f32[2048,512]{1,0:T(8,128)} %param.5, f32[4096]{0:T(1024)S(1)} %fusion.15, f32[]{:T(128)} %bitcast, f32[2048]{0:T(1024)} %param.6), kind=kOutput, calls=%fused_computation.42 | convolution fusion | flops 8641310720 | bytes 41992196 | tf_op jit(solution)/shard_map/nd,kd->nk/dot_general | solution.py:22
  33.4 3.3 pmax.21
  36.7 13.3 %exponential_reduce_fusion.2 = f32[4096]{0:T(1024)S(1)} fusion(f32[4096,2048]{0,1:T(8,128)} %get-tuple-element.13, f32[4096]{0:T(1024)S(1)} %pmax.21), kind=kLoop, calls=%fused_computation.7 | loop fusion | flops 16773120 | bytes 33587200 | tf_op jit(solution)/shard_map/reduce_sum | solution.py:25
  50.0 3.5 psum.63
  53.5 17.6 %fusion.10 = f32[2048,512]{1,0:T(8,128)} fusion(bf16[4096,512]{1,0:T(8,128)(2,1)} %param.4, f32[4096,2048]{0,1:T(8,128)} %get-tuple-element.13, f32[4096]{0:T(1024)S(1)} %log_add_fusion.2), kind=kOutput, calls=%fused_computation.17 | convolution fusion | flops 8606711808 | bytes 41959424 | tf_op jit(solution)/shard_map/nk,nd->kd/dot_general | solution.py:29
  71.1 0.0 all-reduce.4.cloned.1.call-update
  71.1 0.5 all-reduce.6.cloned.1.call-start
  71.6 13.3 %fusion.1 = f32[2048]{0:T(1024)S(1)} fusion(f32[4096,2048]{0,1:T(8,128)} %get-tuple-element.13, f32[4096]{0:T(1024)S(1)} %log_add_fusion.2), kind=kLoop, calls=%fused_computation.10 | loop fusion | flops 16775168 | bytes 33579008 | tf_op jit(solution)/shard_map/reduce_sum | solution.py:28
  85.0 183.5 %psum.64 = f32[2048]{0:T(1024)S(1)} all-reduce(f32[2048]{0:T(1024)S(1)} %fusion.1), channel_id=1, replica_groups=mesh['fit'=1,'comp'=2,'pts'=64] {'pts'}, use_global_device_ids=true, to_apply=%region_6.0 | all-reduce | flops 2048 | bytes 16384 | tf_op jit(solution)/shard_map/psum | solution.py:30
  268.5 0.0 all-reduce.4.cloned.1.call-done
  268.5 2.8 multiply_reduce_fusion.1
  271.3 19.0 %fusion.21 = (f32[4096]{0:T(1024)S(1)}, f32[2048,4096]{1,0:T(8,128)}) fusion(f32[2048]{0:T(1024)S(1)} %multiply_reduce_fusion.1, bf16[4096,512]{1,0:T(8,128)(2,1)} %param.4, f32[2048,512]{1,0:T(8,128)} %all-reduce.4.cloned.1.call-done, f32[2048]{0:T(1024)S(1)} %get-tuple-element.7, f32[4096]{0:T(1024)S(1)} %fusion.15, f32[]{:T(128)} %bitcast.1, ...), kind=kOutput, calls=%fused_computation.43 | convolution fusion | flops 8642359296 | bytes 42000388 | tf_op jit(solution)/shard_map/nd,kd->nk/dot_general | solution.py:22
  290.4 3.3 pmax.22
  293.7 13.3 %exponential_reduce_fusion.1 = f32[4096]{0:T(1024)S(1)} fusion(f32[2048,4096]{1,0:T(8,128)} %get-tuple-element.15, f32[4096]{0:T(1024)S(1)} %pmax.22), kind=kLoop, calls=%fused_computation.1 | loop fusion | flops 16773120 | bytes 33587200 | tf_op jit(solution)/shard_map/reduce_sum | solution.py:25
  307.0 3.5 psum.66
  310.6 17.6 %fusion.8 = f32[2048,512]{1,0:T(8,128)} fusion(bf16[4096,512]{1,0:T(8,128)(2,1)} %param.4, f32[2048,4096]{1,0:T(8,128)} %get-tuple-element.15, f32[4096]{0:T(1024)S(1)} %log_add_fusion.1), kind=kOutput, calls=%fused_computation.16 | convolution fusion | flops 8606711808 | bytes 41959424 | tf_op jit(solution)/shard_map/nk,nd->kd/dot_general | solution.py:29
  328.1 0.0 all-reduce.6.cloned.1.call-update
  328.2 0.2 all-reduce.8.cloned.1.call-start
  328.4 13.3 %fusion.2 = f32[2048]{0:T(1024)S(1)} fusion(f32[2048,4096]{1,0:T(8,128)} %get-tuple-element.15, f32[4096]{0:T(1024)S(1)} %log_add_fusion.1), kind=kLoop, calls=%fused_computation.11 | loop fusion | flops 16775168 | bytes 33579008 | tf_op jit(solution)/shard_map/reduce_sum | solution.py:28
  341.7 174.6 %psum.67 = f32[2048]{0:T(1024)S(1)} all-reduce(f32[2048]{0:T(1024)S(1)} %fusion.2), channel_id=1, replica_groups=mesh['fit'=1,'comp'=2,'pts'=64] {'pts'}, use_global_device_ids=true, to_apply=%region_14.0 | all-reduce | flops 2048 | bytes 16384 | tf_op jit(solution)/shard_map/psum | solution.py:30
  516.3 0.0 all-reduce.6.cloned.1.call-done
  516.3 2.8 multiply_reduce_fusion
  519.2 19.1 %fusion.22 = (f32[4096]{0:T(1024)S(1)}, f32[2048,4096]{1,0:T(8,128)}) fusion(f32[2048]{0:T(1024)S(1)} %multiply_reduce_fusion, bf16[4096,512]{1,0:T(8,128)(2,1)} %param.4, f32[2048,512]{1,0:T(8,128)} %all-reduce.6.cloned.1.call-done, f32[2048]{0:T(1024)S(1)} %get-tuple-element.5, f32[4096]{0:T(1024)S(1)} %fusion.15, f32[]{:T(128)} %bitcast.2, ...), kind=kOutput, calls=%fused_computation.44 | convolution fusion | flops 8642359296 | bytes 42000388 | tf_op jit(solution)/shard_map/nd,kd->nk/dot_general | solution.py:22
  538.2 3.3 pmax.23
  541.6 13.3 %exponential_reduce_fusion = f32[4096]{0:T(1024)S(1)} fusion(f32[2048,4096]{1,0:T(8,128)} %get-tuple-element.17, f32[4096]{0:T(1024)S(1)} %pmax.23), kind=kLoop, calls=%fused_computation | loop fusion | flops 16773120 | bytes 33587200 | tf_op jit(solution)/shard_map/reduce_sum | solution.py:25
  554.9 3.7 psum.69
  558.6 0.0 copy-start
  558.6 17.6 %fusion.6 = f32[2048,512]{1,0:T(8,128)} fusion(bf16[4096,512]{1,0:T(8,128)(2,1)} %param.4, f32[2048,4096]{1,0:T(8,128)} %get-tuple-element.17, f32[4096]{0:T(1024)S(1)} %log_add_fusion), kind=kOutput, calls=%fused_computation.15 | convolution fusion | flops 8606711808 | bytes 41959424 | tf_op jit(solution)/shard_map/nk,nd->kd/dot_general | solution.py:29
  576.2 0.0 all-reduce.8.cloned.1.call-update
  576.2 0.0 copy-done
  576.2 13.3 %fusion.4 = f32[2048]{0:T(1024)S(1)} fusion(f32[2048,4096]{1,0:T(8,128)} %get-tuple-element.17, f32[4096]{0:T(1024)S(1)} %log_add_fusion), kind=kLoop, calls=%fused_computation.13 | loop fusion | flops 16775168 | bytes 33579008 | tf_op jit(solution)/shard_map/reduce_sum | solution.py:28
  589.6 175.9 %psum.71 = f32[2048]{0:T(1024)S(1)} all-reduce(f32[2048]{0:T(1024)S(1)} %fusion.4), channel_id=1, replica_groups=mesh['fit'=1,'comp'=2,'pts'=64] {'pts'}, use_global_device_ids=true, to_apply=%region_23.0 | all-reduce | flops 2048 | bytes 16384 | tf_op jit(solution)/shard_map/psum | solution.py:30
  765.5 0.6 multiply_log_fusion
  766.1 0.0 all-reduce.8.cloned.1.call-done
  766.1 4.5 broadcast_divide_fusion
  (5 shorter events, 0.0 us)
Async XLA Ops:
  7.2 261.3 %all-reduce.4.cloned.1.call-start = ((), (), s32[]{:S(2)}) async-start(), calls=%async_computation | async-start | bytes 8388608 | tf_op jit(solution)/shard_map/psum | solution.py:30
  71.1 445.2 %all-reduce.6.cloned.1.call-start = ((), (), s32[]{:S(2)}) async-start(), calls=%async_computation.1 | async-start | bytes 8388608 | tf_op jit(solution)/shard_map/psum | solution.py:30
  328.2 437.9 %all-reduce.8.cloned.1.call-start = ((), (), s32[]{:S(2)}) async-start(), calls=%async_computation.2 | async-start | bytes 8388608 | tf_op jit(solution)/shard_map/psum | solution.py:30
  558.6 17.6 %copy-start = (f32[4096]{0:T(1024)}, f32[4096]{0:T(1024)S(1)}, u32[]{:S(2)}) copy-start(f32[4096]{0:T(1024)S(1)} %log_add_fusion) | copy-start | bytes 49156
Sparse Core Ops, SparseCore 0:
  71.3 142.2 all-reduce.3
  328.3 133.0 all-reduce.5
  576.4 134.7 all-reduce.7
where the time goes:
time: 786 us; the launch traced here: 777 us
  blocking collectives  555 us (71%)
  matrix products  110 us (14%)
  other arithmetic  96.3 us (12%)
  between operations  14.1 us (2%)
    psum x3, blocking collectives, per_device(): counts, stat_sums = lax.psum((counts, stat_sums), 'pts')  534 us
    dot_general x3, matrix products, per_device(): jnp.einsum('nd,kd->nk', points, mean_bf, preferred_element_type=jnp.float32)  57.3 us
    dot_general x3, matrix products, per_device(): jnp.einsum('nk,nd->kd', resp_prob.astype(jnp.bfloat16), points, preferred...  52.7 us
    reduce_sum x3, other arithmetic, per_device(): counts = jnp.sum(resp_prob, axis=0)  39.9 us
    reduce_sum x3, other arithmetic, per_device(): jnp.sum(jnp.exp(logits - row_top[:, None]), axis=1)  39.8 us
  transfers between devices with their start and end apart: 3, of which 0 were waited for; matrix products, arithmetic and copies ran while one was open for 5% of the time, Pallas kernels for 0%

commit v1 on v0

v1 whole, which is shorter than its diff:
```python
import functools
import math

import jax
import jax.numpy as jnp
from jax import lax
from jax.experimental import pallas as pl
from jax.experimental.pallas import tpu as pltpu
from jax.sharding import PartitionSpec as P

PRIOR_ALPHA = 1e-3
COUNT_EPS = 1e-6
LOG2E = math.log2(math.e)
LN2 = math.log(2.0)
F32, BF16 = jnp.float32, jnp.bfloat16
MESH = pl.DeviceIdType.MESH

AXES = {"z": 1, "y": 2, "x": 3}
ORDERS = (("x", "y", "z"), ("y", "z", "x"), ("z", "x", "y"))
SUM_TILES = ((0, 6), (6, 11), (11, 17))
BF_TILES = ((0, 3), (3, 6), (6, 8))
PB = 256
KC = 512


def cat(parts, axis):
    return jnp.concatenate(parts, axis=axis)


def kernel(n_total, k_total, sweeps, x_hbm, mu_hbm, ct_hbm, beta_ref, out_mu, out_ct, out_lse,
           xv, e_ref, l0, l1, s_ref, muf, mu, ct, hrep, lrep, st, stp, wrow, qh,
           ra0, ra1, ra2, rb0, rb1, rb2, rc0, rc1, rc2,
           load_sem, ex_send, ex_recv, rs_send, rs_recv, ag_send, ag_recv):
    n_pts = xv.shape[0]
    nb = n_pts // PB
    fit, comp, pts = lax.axis_index("fit"), lax.axis_index("comp"), lax.axis_index("pts")
    me = {"z": lax.div(pts, 16), "y": lax.rem(lax.div(pts, 4), 4), "x": lax.rem(pts, 4)}
    right = {d: lax.rem(me[d] + 1, 4) for d in me}
    left = {d: lax.rem(me[d] + 3, 4) for d in me}
    over = {d: lax.rem(me[d] + 2, 4) for d in me}
    bufs = ((ra0, ra1, ra2), (rb0, rb1, rb2), (rc0, rc1, rc2))

    def dev(d, v):
        c = dict(me)
        c[d] = v
        return (fit, comp, c["z"] * 16 + c["y"] * 4 + c["x"])

    def where_at(ts, sel):
        return (pl.ds(ts[0], ts[1] - ts[0]),) + tuple(sel.get(d, slice(None)) for d in ("z", "y", "x"))

    def remote(src, dst, ss, rs, device):
        return pltpu.make_async_remote_copy(src_ref=src, dst_ref=dst, send_sem=ss, recv_sem=rs,
                                            device_id=device, device_id_type=MESH)

    def half(i):
        return pl.ds(2 * i, 2)

    def reduce_phase(k):
        pend = []
        for p, order in enumerate(ORDERS):
            d, ts, buf = order[k], SUM_TILES[p], bufs[k][p]
            fixed = {order[j]: me[order[j]] for j in range(k)}

            def copy(i, src, device, p=p, buf=buf):
                c = remote(src, buf.at[i], rs_send.at[p, k, i], rs_recv.at[p, k, i], device)
                c.start()
                return c

            if k == 2:
                blk = lambda v, fixed=fixed, d=d, ts=ts: s_ref.at[where_at(ts, {**fixed, d: v})]
                cs = [copy(2, blk(over[d]), dev(d, over[d])), copy(0, blk(right[d]), dev(d, right[d])),
                      copy(1, blk(left[d]), dev(d, left[d]))]
                pend.append(cs)
                continue

            def at(v, h, fixed=fixed, d=d, ts=ts, order=order):
                return where_at(ts, {**fixed, d: v, order[2]: half(h)})

            to_r, to_l = dev(d, right[d]), dev(d, left[d])
            c0 = copy(0, s_ref.at[at(over[d], 0)], to_r)
            c1 = copy(1, s_ref.at[at(over[d], 1)], to_l)
            c3 = copy(3, s_ref.at[at(right[d], 1)], to_r)
            c4 = copy(4, s_ref.at[at(left[d], 0)], to_l)
            pend.append((c0, c1, c3, c4, at, copy))
        if k == 2:
            for p, order in enumerate(ORDERS):
                ts, buf = SUM_TILES[p], bufs[k][p]
                for c in pend[p]:
                    c.wait()
                own = where_at(ts, me)
                s_ref[own] = (s_ref[own] + buf[0]) + (buf[1] + buf[2])
            return
        fwd = []
        for p, order in enumerate(ORDERS):
            d, buf = order[k], bufs[k][p]
            c0, c1, c3, c4, at, copy = pend[p]
            c0.wait_recv()
            buf[0] = buf[0] + s_ref[at(right[d], 0)]
            c2 = copy(2, buf.at[0], dev(d, right[d]))
            c1.wait_recv()
            buf[1] = buf[1] + s_ref[at(left[d], 1)]
            c5 = copy(5, buf.at[1], dev(d, left[d]))
            fwd.append((c2, c5))
        for p, order in enumerate(ORDERS):
            d, buf = order[k], bufs[k][p]
            c0, c1, c3, c4, at, copy = pend[p]
            c2, c5 = fwd[p]
            c4.wait_recv()
            c2.wait_recv()
            s_ref[at(me[d], 0)] = s_ref[at(me[d], 0)] + (buf[2] + buf[4])
            c3.wait_recv()
            c5.wait_recv()
            s_ref[at(me[d], 1)] = s_ref[at(me[d], 1)] + (buf[3] + buf[5])
            for c in (c0, c1, c3, c4, c2, c5):
                c.wait_send()

    def gather_phase(k, blocks):
        def view(ref, ts, sel):
            w = where_at(ts or (0, 1), sel)
            return ref.at[w] if ts else ref.at[w[1:]]

        pend = []
        for p, order in enumerate(ORDERS):
            d = order[k]
            fixed = {order[j]: me[order[j]] for j in range(k)}
            for q, (ref, ts) in enumerate(blocks[p]):
                def copy(i, sel, device, p=p, q=q, ref=ref, ts=ts):
                    v = view(ref, ts, sel)
                    c = remote(v, v, ag_send.at[p, q, k, i], ag_recv.at[p, q, k, i], device)
                    c.start()
                    return c

                to_r, to_l, to_o = dev(d, right[d]), dev(d, left[d]), dev(d, over[d])
                if k == 2:
                    sel = {**fixed, d: me[d]}
                    pend.append((copy(0, sel, to_o), copy(1, sel, to_r), copy(2, sel, to_l)))
                    continue

                def sel(v, h, fixed=fixed, d=d, order=order):
                    return {**fixed, d: v, order[2]: half(h)}

                c0 = copy(0, sel(me[d], 0), to_r)
                c1 = copy(1, sel(me[d], 1), to_l)
                c2 = copy(2, sel(me[d], 1), to_r)
                c3 = copy(3, sel(me[d], 0), to_l)
                pend.append((d, c0, c1, c2, c3, sel, copy, to_r, to_l))
        if k == 2:
            for cs in pend:
                for c in cs:
                    c.wait()
            return
        fwd = []
        for d, c0, c1, c2, c3, sel, copy, to_r, to_l in pend:
            c0.wait_recv()
            c4 = copy(4, sel(left[d], 0), to_r)
            c1.wait_recv()
            c5 = copy(5, sel(right[d], 1), to_l)
            fwd.append((c4, c5))
        for (d, c0, c1, c2, c3, *_), (c4, c5) in zip(pend, fwd):
            for c in (c2, c3, c4, c5):
                c.wait_recv()
            for c in (c0, c1, c2, c3, c4, c5):
                c.wait_send()

    lane = lax.broadcasted_iota(jnp.int32, (8, 128), 1)

    def expand():
        t = ct[...].reshape(512, 128)
        for r4 in range(4):
            hrep[r4] = jnp.broadcast_to(t[:, 16 * r4:16 * r4 + 1], (512, 128))
            lrep[r4] = jnp.broadcast_to(t[:, 64 + 16 * r4:65 + 16 * r4], (512, 128)) * LOG2E

    def logits(j, lref, b2):
        cols = pl.ds(pl.multiple_of(j * PB, PB), PB)
        xj = xv[cols, :]
        q = qh[:, cols]
        top = None
        for r2 in range(2):
            rows = cat([mu[r2 * 4 + c].reshape(1024, 128) for c in range(4)], 1)
            a = lax.dot_general(rows, xj, (((1,), (1,)), ((), ())), preferred_element_type=F32)
            a = a.reshape(64, 2, 8, PB)
            for h in range(2):
                r4 = r2 * 2 + h
                hh = cat([hrep[r4]] * (PB // 128), 1)
                ll = cat([lrep[r4]] * (PB // 128), 1)
                v = ((a[:, h].reshape(512, PB) - hh) - q) * b2 + ll
                lref[r4] = v
                t = jnp.max(v.reshape(64, 8, PB), axis=0)
                top = t if top is None else jnp.maximum(top, t)
        st[0:1, cols] = jnp.max(top, axis=0, keepdims=True)

    def exps(j, lref):
        cols = pl.ds(pl.multiple_of(j * PB, PB), PB)
        m = st[0:1, cols]
        tot = None
        for r4 in range(4):
            e = jnp.exp2(lref[r4] - m)
            e_ref[r4, :, cols] = e
            t = jnp.sum(e.reshape(64, 8, PB), axis=0)
            tot = t if tot is None else tot + t
        st[1:2, cols] = jnp.sum(tot, axis=0, keepdims=True)

    cx = pltpu.make_async_copy(x_hbm, xv, load_sem.at[0])
    cm = pltpu.make_async_copy(mu_hbm, mu, load_sem.at[1])
    cc = pltpu.make_async_copy(ct_hbm, ct, load_sem.at[2])
    cx.start()
    cm.start()
    cc.start()
    cx.wait()
    cm.wait()
    cc.wait()

    @pl.loop(0, n_pts // 128)
    def _(i):
        rows = pl.ds(pl.multiple_of(i * 128, 128), 128)
        xb = xv[rows, :].astype(F32)
        sq = xb * xb
        sq = (sq[:, 0:128] + sq[:, 128:256]) + (sq[:, 256:384] + sq[:, 384:512])
        qh[:, rows] = jnp.sum(sq.T, axis=0, keepdims=True) * 0.5

    st[...] = jnp.zeros_like(st)

    @pl.loop(0, sweeps)
    def _(sweep):
        b2 = beta_ref[sweep] * (2.0 * LOG2E)
        expand()
        logits(0, l0, b2)

        @pl.loop(0, nb // 2 - 1)
        def _(i):
            logits(2 * i + 1, l1, b2)
            exps(2 * i, l0)
            logits(2 * i + 2, l0, b2)
            exps(2 * i + 1, l1)

        logits(nb - 1, l1, b2)
        exps(nb - 2, l0)
        exps(nb - 1, l1)

        slot = lax.rem(sweep, 2)
        ex = remote(st, stp.at[slot], ex_send, ex_recv.at[slot], (fit, 1 - comp, pts))
        ex.start()
        s_ref[16] = jnp.zeros((4, 4, 4, 8, 128), F32)
        ex.wait()
        ma, mb = st[0:1, :], stp[slot, 0:1, :]
        mm = jnp.maximum(ma, mb)
        tot = st[1:2, :] * jnp.exp2(ma - mm) + stp[slot, 1:2, :] * jnp.exp2(mb - mm)
        lse2 = mm + jnp.log2(tot)
        wrow[...] = jnp.exp2(ma - lse2)
        out_lse[...] = lse2 * LN2

        @pl.loop(0, 4)
        def _(r4):
            acc, cnt = None, None
            for kc in range(n_pts // KC):
                k0 = kc * KC
                r = e_ref[r4, :, k0:k0 + KC] * wrow[:, k0:k0 + KC]
                for t in range(KC // 128):
                    rt = r[:, t * 128:(t + 1) * 128]
                    cnt = rt if cnt is None else cnt + rt
                part = jnp.dot(r.astype(BF16), xv[k0:k0 + KC, :], preferred_element_type=F32)
                acc = part if acc is None else acc + part
            for c in range(4):
                s_ref[r4 * 4 + c] = acc[:, c * 128:(c + 1) * 128].reshape(4, 4, 4, 8, 128)
            cb = jnp.broadcast_to(jnp.sum(cnt, axis=1, keepdims=True), (512, 128)).reshape(64, 8, 128)
            cb = jnp.where((lane >= 32 * r4) & (lane < 32 * r4 + 32), cb, 0.0)
            s_ref[16] = s_ref[16] + cb.reshape(4, 4, 4, 8, 128)

        for k in range(3):
            reduce_phase(k)

        at = (me["z"], me["y"], me["x"])
        ntile = s_ref[(16,) + at]
        vals, tile = [], jnp.zeros((8, 128), F32)
        for r4 in range(4):
            n = jnp.broadcast_to(ntile[:, 32 * r4:32 * r4 + 1], (8, 128))
            row = [s_ref[(r4 * 4 + c,) + at] / (n + COUNT_EPS) for c in range(4)]
            vals.append(row)
            sq = (row[0] * row[0] + row[1] * row[1]) + (row[2] * row[2] + row[3] * row[3])
            hh = jnp.broadcast_to(0.5 * jnp.sum(sq, axis=1, keepdims=True), (8, 128))
            lw = jnp.log((n + PRIOR_ALPHA) / (n_total + k_total * PRIOR_ALPHA))
            tile = jnp.where(lax.div(lane, 16) == r4, hh, tile)
            tile = jnp.where(lax.div(lane, 16) == 4 + r4, lw, tile)

        @pl.when(sweep < sweeps - 1)
        def _():
            for r2 in range(2):
                for c in range(4):
                    mu[(r2 * 4 + c,) + at] = cat([vals[2 * r2][c], vals[2 * r2 + 1][c]], 0).astype(BF16)
            ct[at] = tile
            blocks = [[(mu, BF_TILES[0])], [(mu, BF_TILES[1])], [(mu, BF_TILES[2]), (ct, None)]]
            for k in (2, 1, 0):
                gather_phase(k, blocks)

        @pl.when(sweep == sweeps - 1)
        def _():
            for r4 in range(4):
                for c in range(4):
                    muf[(r4 * 4 + c,) + at] = vals[r4][c]
            muf[(16,) + at] = tile
            blocks = [[(muf, SUM_TILES[p])] for p in range(3)]
            for k in (2, 1, 0):
                gather_phase(k, blocks)

    o0 = pltpu.make_async_copy(muf.at[pl.ds(0, 16)], out_mu, load_sem.at[0])
    o1 = pltpu.make_async_copy(muf.at[16], out_ct, load_sem.at[1])
    o0.start()
    o1.start()
    o0.wait()
    o1.wait()


def solution(mesh):
    row_groups = mesh.shape["pts"]
    comp_groups = mesh.shape["comp"]

    def per_device(points, mean_vecs, log_w, inv_temp):
        n_pts = points.shape[0]
        n_total = n_pts * row_groups
        k_total = mean_vecs.shape[0] * comp_groups
        sweeps = inv_temp.shape[0]
        mu_in = mean_vecs.astype(BF16).reshape(64, 2, 16, 4, 128).transpose(1, 3, 0, 2, 4)
        mu_in = mu_in.reshape(8, 4, 4, 4, 16, 128)
        sq = 0.5 * jnp.sum(mean_vecs * mean_vecs, axis=1)
        both = cat([v.reshape(64, 4, 8).transpose(0, 2, 1) for v in (sq, log_w)], 2)
        ct_in = jnp.broadcast_to(both[..., None], (64, 8, 8, 16)).reshape(4, 4, 4, 8, 128)

        def rbuf(k):
            shapes = []
            for (lo, hi), order in zip(SUM_TILES, ORDERS):
                if k == 2:
                    shapes.append(pltpu.VMEM((3, hi - lo, 8, 128), F32))
                    continue
                dims = [2 if d == order[2] else 4 for d in ("z", "y", "x") if d not in order[:k + 1]]
                shapes.append(pltpu.VMEM((6, hi - lo, *dims, 8, 128), F32))
            return shapes

        any_spec = pl.BlockSpec(memory_space=pl.ANY)
        out_mu, out_ct, out_lse = pl.pallas_call(
            functools.partial(kernel, n_total, k_total, sweeps),
            out_shape=(jax.ShapeDtypeStruct((16, 4, 4, 4, 8, 128), F32),
                       jax.ShapeDtypeStruct((4, 4, 4, 8, 128), F32),
                       jax.ShapeDtypeStruct((1, n_pts), F32)),
            in_specs=[any_spec, any_spec, any_spec, pl.BlockSpec(memory_space=pltpu.SMEM)],
            out_specs=(any_spec, any_spec, pl.BlockSpec(memory_space=pltpu.VMEM)),
            scratch_shapes=[
                pltpu.VMEM((n_pts, 512), BF16),
                pltpu.VMEM((4, 512, n_pts), F32),
                pltpu.VMEM((4, 512, PB), F32),
                pltpu.VMEM((4, 512, PB), F32),
                pltpu.VMEM((17, 4, 4, 4, 8, 128), F32),
                pltpu.VMEM((17, 4, 4, 4, 8, 128), F32),
                pltpu.VMEM((8, 4, 4, 4, 16, 128), BF16),
                pltpu.VMEM((4, 4, 4, 8, 128), F32),
                pltpu.VMEM((4, 512, 128), F32),
                pltpu.VMEM((4, 512, 128), F32),
                pltpu.VMEM((8, n_pts), F32),
                pltpu.VMEM((2, 8, n_pts), F32),
                pltpu.VMEM((1, n_pts), F32),
                pltpu.VMEM((1, n_pts), F32),
                *rbuf(0), *rbuf(1), *rbuf(2),
                pltpu.SemaphoreType.DMA((3,)),
                pltpu.SemaphoreType.DMA,
                pltpu.SemaphoreType.DMA((2,)),
                pltpu.SemaphoreType.DMA((3, 3, 6)),
                pltpu.SemaphoreType.DMA((3, 3, 6)),
                pltpu.SemaphoreType.DMA((3, 2, 3, 6)),
                pltpu.SemaphoreType.DMA((3, 2, 3, 6)),
            ],
            compiler_params=pltpu.CompilerParams(has_side_effects=True, vmem_limit_bytes=67043328),
            cost_estimate=pl.CostEstimate(flops=6 * 2 * n_pts * 2048 * 512, bytes_accessed=1 << 24, transcendentals=0),
        )(points, mu_in, ct_in, inv_temp)
        means = out_mu.reshape(4, 4, 64, 8, 128).transpose(2, 0, 3, 1, 4).reshape(2048, 512)
        logw = out_ct.reshape(64, 8, 8, 16)[:, :, 4:, 0].transpose(0, 2, 1).reshape(2048)
        return means, logw, out_lse.reshape(n_pts)

    row_spec = P(("fit", "pts"))
    comp_spec = P(("fit", "comp"))
    return jax.shard_map(
        per_device,
        mesh=mesh,
        in_specs=(P(("fit", "pts"), None), P(("fit", "comp"), None), comp_spec, P()),
        out_specs=(P(("fit", "comp"), None), comp_spec, row_spec),
        check_vma=False,
    )
```

time: 786 us -> 267 us (0.34); the launches traced: 777 us -> 267 us
  blocking collectives: 555 us -> 0 us
  Pallas kernels: 0 us -> 246 us
  matrix products: 110 us -> 0 us
  other arithmetic: 96.3 us -> 5.44 us
  local copies, waits for them, and re-layouts: 1.37 us -> 15.1 us
  between operations: 14.1 us -> 0.71 us
    psum x6 -> x0, blocking collectives: 545 us -> none  [the longest x3 534 us: per_device(): counts, stat_sums = lax.psum((counts, stat_sums), 'pts')]
    pallas_call x0 -> x1, Pallas kernels: none -> 246 us  [per_device(): pl.pallas_call(functools.partial(kernel, n_total, k_total, sweeps), out_s...]
    dot_general x6 -> x0, matrix products: 110 us -> none  [the longest x3 57.3 us: per_device(): jnp.einsum('nd,kd->nk', points, mean_bf, preferred_element_type=jnp.float32)]
    reduce_sum x9 -> x1, other arithmetic: 88 us -> 5.36 us  [per_device(): sq = 0.5 * jnp.sum(mean_vecs * mean_vecs, axis=1)]
    pmax x3 -> x0, blocking collectives: 10 us -> none  [per_device(): row_top = lax.pmax(jnp.max(logits, axis=1), 'comp')]
  transfers between devices with their start and end apart: 3 -> 0, of which waited for: 0 -> 0; matrix products, arithmetic and copies ran while one was open for 5% -> 0% of each run, Pallas kernels for 0% -> 0%
where the time goes in v1:
time: 267 us
  Pallas kernels  246 us (92%)
  local copies, waits for them, and re-layouts  15.1 us (6%)
  other arithmetic  5.44 us (2%)
    pallas_call x1, Pallas kernels, per_device(): pl.pallas_call(functools.partial(kernel, n_total, k_total, sweeps), out_s...  246 us
    reduce_sum x1, other arithmetic, per_device(): sq = 0.5 * jnp.sum(mean_vecs * mean_vecs, axis=1)  5.36 us

profile of v1, /device:TPU:0, one launch (start us, length us, event | category | flops | bytes accessed | tf_op | source)
XLA Modules:
  0.0 266.9 jit_solution(6090531125590667102)
XLA Ops:
  0.6 0.9 reshape.40
  1.5 5.4 %multiply_reduce_fusion = (f32[2048]{0:T(1024)S(1)}, bf16[2048,512]{1,0:T(8,128)(2,1)}) fusion(f32[2048,512]{1,0:T(8,128)} %param.5), kind=kLoop, calls=%fused_computation | loop fusion | flops 3143680 | bytes 6299648 | tf_op jit(solution)/shard_map/reduce_sum | solution.py:324
  6.9 0.2 mul.16
  7.1 0.1 pad_maximum_fusion
  7.2 0.1 copy.22
  7.3 0.6 broadcast_in_dim.2
  7.9 1.3 reshape.41.ct_hbm
  9.2 2.5 reshape.38
  11.7 1.6 copy.21
  13.3 245.7 %shard_map.67 = (f32[16,4,4,4,8,128]{5,4,3,2,1,0:T(8,128)}, f32[4,4,4,8,128]{4,3,2,1,0:T(8,128)}, f32[1,4096]{1,0:T(1,128)}) custom-call(bf16[4096,512]{1,0:T(8,128)(2,1)} %x_hbm.1, bf16[8,4,4,4,16,128]{5,4,3,2,1,0:T(8,128)(2,1)} %bitcast.19, f32[4,4,4,8,128]{4,3,2,1,0:T(8,128)} %reshape.41.ct_hbm, f32[3]{0:T(128)} %beta_ref.1), custom_call_target="tpu_custom_call" | custom-call | flops 51539607552 | bytes 16777216 | tf_op jit(solution)/shard_map/pallas_call | solution.py:339
  259.0 0.0 copy-start
  259.0 4.8 %copy.23 = f32[64,4,8,4,128]{4,2,3,1,0:T(8,128)} copy(f32[64,4,8,4,128]{4,2,0,3,1:T(8,128)} %bitcast.18) | data formatting | bytes 8388608 | tf_op jit(solution)/shard_map/transpose | solution.py:373
  263.8 0.0 copy-start.1
  263.8 0.0 copy-done
  263.8 0.6 reshape.44
  264.4 0.3 slice.4
  264.8 0.7 copy.24
  265.4 0.1 copy.25
  265.6 0.8 reshape.45
  266.3 0.0 copy-done.1
  266.3 0.6 copy.27
  (1 shorter events, 0.0 us)
Async XLA Ops:
  259.0 4.9 %copy-start = (f32[4,4,4,8,128]{4,3,2,1,0:T(8,128)S(1)}, f32[4,4,4,8,128]{4,3,2,1,0:T(8,128)}, u32[]{:S(2)}) copy-start(f32[4,4,4,8,128]{4,3,2,1,0:T(8,128)} %get-tuple-element.7) | copy-start | bytes 786436
  263.8 2.5 copy-start.1

commit v2 on v0

v2 whole, which is shorter than its diff:
```python
import functools
import math

import jax
import jax.numpy as jnp
from jax import lax
from jax.experimental import pallas as pl
from jax.experimental.pallas import tpu as pltpu
from jax.sharding import PartitionSpec as P

PRIOR_ALPHA = 1e-3
COUNT_EPS = 1e-6
LOG2E = math.log2(math.e)
LN2 = math.log(2.0)
F32, BF16 = jnp.float32, jnp.bfloat16
MESH = pl.DeviceIdType.MESH

DIMS = ("z", "y", "x")
ORDERS = (("x", "y", "z"), ("y", "z", "x"), ("z", "x", "y"))
SUM_TILES = ((0, 3), (3, 6), (6, 9))
BF_TILES = (((0, 2), (2, 3), (3, 4)), ((0, 1), (1, 2), (2, 4)))
PB = 512
KC = 512


def cat(parts, axis):
    return jnp.concatenate(parts, axis=axis)


def kernel(n_total, k_total, sweeps, x_hbm, mean_hbm, lw_ref, beta_ref, out_mu, out_lw, out_lse,
           xv, e_ref, l0, l1, s_ref, muf, mu, ct, hrep, lrep, st, stp, wrow, qh,
           ra0, ra1, ra2, rb0, rb1, rb2, rc0, rc1, rc2,
           load_sem, ex_send, ex_recv, rs_send, rs_recv, ag_send, ag_recv):
    n_pts = xv.shape[0]
    nb = n_pts // PB
    fit, comp, pts = lax.axis_index("fit"), lax.axis_index("comp"), lax.axis_index("pts")
    me = {"z": lax.div(pts, 16), "y": lax.rem(lax.div(pts, 4), 4), "x": lax.rem(pts, 4)}
    near = {r: {d: lax.rem(me[d] + r, 4) for d in DIMS} for r in (1, 2, 3)}
    bufs = ((ra0, ra1, ra2), (rb0, rb1, rb2), (rc0, rc1, rc2))
    own = (me["z"], me["y"], me["x"])
    lane = lax.broadcasted_iota(jnp.int32, (8, 128), 1)

    def dev(d, r):
        c = {**me, d: near[r][d]}
        return (fit, comp, c["z"] * 16 + c["y"] * 4 + c["x"])

    def coord(d, r):
        return near[r][d] if r else me[d]

    def place(p, k, r, half=None):
        order = ORDERS[p]
        sel = {order[j]: me[order[j]] for j in range(k)}
        sel[order[k]] = coord(order[k], r)
        if half is not None:
            sel[order[2]] = pl.ds(2 * half, 2)
        return tuple(sel.get(d, slice(None)) for d in DIMS)

    def remote(src, dst, ss, rs, device):
        return pltpu.make_async_remote_copy(src_ref=src, dst_ref=dst, send_sem=ss, recv_sem=rs,
                                            device_id=device, device_id_type=MESH)

    def sums(h, p):
        return (h, pl.ds(SUM_TILES[p][0], SUM_TILES[p][1] - SUM_TILES[p][0]))

    def rs_copy(h, p, k, i):
        d, buf = ORDERS[p][k], bufs[k][p]
        if k == 2:
            r = (1, 3, 2)[i]
            src = s_ref.at[sums(h, p) + place(p, k, r)]
        else:
            r = (1, 3, 1, 1, 3, 3)[i]
            if i in (2, 5):
                src = buf.at[h, 0 if i == 2 else 1]
            else:
                to, half = {0: (2, 0), 1: (2, 1), 3: (1, 1), 4: (3, 0)}[i]
                src = s_ref.at[sums(h, p) + place(p, k, to, half)]
        j = 6 * k + i
        return remote(src, buf.at[h, i], rs_send.at[h, p, j], rs_recv.at[h, p, j], dev(d, r))

    def rs_start(h, k):
        for i in ((2, 0, 1) if k == 2 else (0, 1, 3, 4)):
            for p in range(3):
                rs_copy(h, p, k, i).start()

    def rs_relay(h, k):
        for p in range(3):
            buf = bufs[k][p]
            for i, to, half, nxt in ((0, 1, 0, 2), (1, 3, 1, 5)):
                rs_copy(h, p, k, i).wait_recv()
                buf[h, i] = buf[h, i] + s_ref[sums(h, p) + place(p, k, to, half)]
                rs_copy(h, p, k, nxt).start()

    def rs_finish(h, k):
        for p in range(3):
            buf = bufs[k][p]
            if k == 2:
                for i in range(3):
                    rs_copy(h, p, k, i).wait()
                mine = sums(h, p) + own
                s_ref[mine] = (s_ref[mine] + buf[h, 0]) + (buf[h, 1] + buf[h, 2])
                continue
            for half, i, j in ((0, 2, 4), (1, 3, 5)):
                rs_copy(h, p, k, i).wait_recv()
                rs_copy(h, p, k, j).wait_recv()
                mine = sums(h, p) + place(p, k, 0, half)
                s_ref[mine] = s_ref[mine] + (buf[h, i] + buf[h, j])
            for i in range(6):
                rs_copy(h, p, k, i).wait_send()

    def bf_units(h):
        units = []
        for p, (lo, hi) in enumerate(BF_TILES[h]):
            units.append((mu, (h, pl.ds(lo, hi - lo)), p))
        return units + [(ct, (h,), 1)]

    def f32_units(h):
        return [(muf, sums(h, p), p) for p in range(3)]

    def ag_copy(units, h, u, k, i):
        ref, lead, p = units[u]
        d = ORDERS[p][k]
        if k == 2:
            r = (1, 3, 2)[i]
            view = ref.at[lead + place(p, k, 0)]
        else:
            frm, half, r = ((0, 0, 1), (0, 1, 3), (0, 1, 1), (0, 0, 3), (3, 0, 1), (1, 1, 3))[i]
            view = ref.at[lead + place(p, k, frm, half)]
        j = 6 * k + i
        return remote(view, view, ag_send.at[h, u, j], ag_recv.at[h, u, j], dev(d, r))

    def ag_start(units, h, k):
        for i in ((2, 0, 1) if k == 2 else range(4)):
            for u in range(len(units)):
                ag_copy(units, h, u, k, i).start()

    def ag_relay(units, h, k):
        for u in range(len(units)):
            for i, nxt in ((0, 4), (1, 5)):
                ag_copy(units, h, u, k, i).wait_recv()
                ag_copy(units, h, u, k, nxt).start()

    def ag_finish(units, h, k):
        for u in range(len(units)):
            if k == 2:
                for i in range(3):
                    ag_copy(units, h, u, k, i).wait()
                continue
            for i in range(2, 6):
                ag_copy(units, h, u, k, i).wait_recv()
            for i in range(6):
                ag_copy(units, h, u, k, i).wait_send()

    def column(v, lanes):
        return jnp.broadcast_to(v[:, lanes:lanes + 1], (v.shape[0], 128))

    def expand(h):
        t = ct[h].reshape(512, 128)
        for hh in range(2):
            hrep[h, hh] = column(t, 32 * hh)
            lrep[h, hh] = column(t, 64 + 32 * hh) * LOG2E

    def logits(h, j, lref, b2):
        cols = pl.ds(pl.multiple_of(j * PB, PB), PB)
        xj = xv[cols, :]
        q = qh[:, cols]
        rows = cat([mu[h, c].reshape(1024, 128) for c in range(4)], 1)
        a = lax.dot_general(rows, xj, (((1,), (1,)), ((), ())), preferred_element_type=F32)
        a = a.reshape(64, 2, 8, PB)
        top = None
        for hh in range(2):
            hc = cat([hrep[h, hh]] * (PB // 128), 1)
            lc = cat([lrep[h, hh]] * (PB // 128), 1)
            v = ((a[:, hh].reshape(512, PB) - hc) - q) * b2 + lc
            lref[hh] = v
            t = jnp.max(v.reshape(64, 8, PB), axis=0)
            top = t if top is None else jnp.maximum(top, t)
        st[2 * h, :, cols] = jnp.max(top, axis=0, keepdims=True)

    def exps(h, j, lref):
        cols = pl.ds(pl.multiple_of(j * PB, PB), PB)
        m = st[2 * h, :, cols]
        tot = None
        for hh in range(2):
            e = jnp.exp2(lref[hh] - m)
            e_ref[2 * h + hh, :, cols] = e
            t = jnp.sum(e.reshape(64, 8, PB), axis=0)
            tot = t if tot is None else tot + t
        st[2 * h + 1, :, cols] = jnp.sum(tot, axis=0, keepdims=True)

    def scores(h, b2, during=()):
        logits(h, 0, l0, b2)

        @pl.loop(0, nb // 2 - 1)
        def _(i):
            for n, step in enumerate(during):
                pl.when(i == n)(step)
            logits(h, 2 * i + 1, l1, b2)
            exps(h, 2 * i, l0)
            logits(h, 2 * i + 2, l0, b2)
            exps(h, 2 * i + 1, l1)

        logits(h, nb - 1, l1, b2)
        exps(h, nb - 2, l0)
        exps(h, nb - 1, l1)

    def normalise(slot):
        ex = remote(st, stp.at[slot], ex_send, ex_recv.at[slot], (fit, 1 - comp, pts))
        ex.start()
        for h in range(2):
            s_ref[h, 8] = jnp.zeros((4, 4, 4, 8, 128), F32)
        ex.wait()
        tops = [st[0], st[2], stp[slot, 0], stp[slot, 2]]
        mm = jnp.maximum(jnp.maximum(tops[0], tops[1]), jnp.maximum(tops[2], tops[3]))
        tot = (st[1] * jnp.exp2(tops[0] - mm) + st[3] * jnp.exp2(tops[1] - mm)) + (
            stp[slot, 1] * jnp.exp2(tops[2] - mm) + stp[slot, 3] * jnp.exp2(tops[3] - mm))
        lse2 = mm + jnp.log2(tot)
        for h in range(2):
            wrow[h] = jnp.exp2(tops[h] - lse2)
        return lse2

    def moments():
        @pl.loop(0, 4)
        def _(r4):
            h, hh = lax.div(r4, 2), lax.rem(r4, 2)
            pl.when(r4 == 2)(lambda: rs_start(0, 0))
            pl.when(r4 == 3)(lambda: rs_relay(0, 0))
            acc, cnt = None, None
            for kc in range(n_pts // KC):
                k0 = kc * KC
                r = e_ref[r4, :, k0:k0 + KC] * wrow[h, :, k0:k0 + KC]
                for t in range(KC // 128):
                    rt = r[:, t * 128:(t + 1) * 128]
                    cnt = rt if cnt is None else cnt + rt
                part = jnp.dot(r.astype(BF16), xv[k0:k0 + KC, :], preferred_element_type=F32)
                acc = part if acc is None else acc + part
            for c in range(4):
                s_ref[h, hh * 4 + c] = acc[:, c * 128:(c + 1) * 128].reshape(4, 4, 4, 8, 128)
            cb = jnp.broadcast_to(jnp.sum(cnt, axis=1, keepdims=True), (512, 128)).reshape(64, 8, 128)
            cb = jnp.where(lax.div(lane, 64) == hh, cb, 0.0)
            s_ref[h, 8] = s_ref[h, 8] + cb.reshape(4, 4, 4, 8, 128)

    def update(h):
        ntile = s_ref[(h, 8) + own]
        vals, tile = [], jnp.zeros((8, 128), F32)
        for hh in range(2):
            n = column(ntile, 64 * hh)
            row = [s_ref[(h, hh * 4 + c) + own] / (n + COUNT_EPS) for c in range(4)]
            vals.append(row)
            sq = (row[0] * row[0] + row[1] * row[1]) + (row[2] * row[2] + row[3] * row[3])
            hc = jnp.broadcast_to(0.5 * jnp.sum(sq, axis=1, keepdims=True), (8, 128))
            lw = jnp.log((n + PRIOR_ALPHA) / (n_total + k_total * PRIOR_ALPHA))
            tile = jnp.where(lax.div(lane, 32) == hh, hc, tile)
            tile = jnp.where(lax.div(lane, 32) == 2 + hh, lw, tile)
        return vals, tile

    def update_bf(h):
        vals, tile = update(h)
        for c in range(4):
            mu[(h, c) + own] = cat([vals[0][c], vals[1][c]], 0).astype(BF16)
        ct[(h,) + own] = tile

    def update_f32(h):
        vals, tile = update(h)
        for hh in range(2):
            for c in range(4):
                muf[(h, hh * 4 + c) + own] = vals[hh][c]
        muf[(h, 8) + own] = tile

    def exchange(units, upd):
        u0, u1 = units
        rs_start(1, 0)
        rs_finish(0, 0)
        rs_start(0, 1)
        rs_relay(1, 0)
        rs_relay(0, 1)
        rs_finish(0, 1)
        rs_start(0, 2)
        rs_finish(1, 0)
        rs_start(1, 1)
        rs_finish(0, 2)
        upd(0)
        ag_start(u0, 0, 2)
        rs_relay(1, 1)
        ag_finish(u0, 0, 2)
        ag_start(u0, 0, 1)
        rs_finish(1, 1)
        rs_start(1, 2)
        ag_relay(u0, 0, 1)
        ag_finish(u0, 0, 1)
        ag_start(u0, 0, 0)
        rs_finish(1, 2)
        upd(1)
        ag_start(u1, 1, 2)
        ag_relay(u0, 0, 0)
        ag_finish(u1, 1, 2)
        ag_start(u1, 1, 1)
        ag_finish(u0, 0, 0)

    loads = [pltpu.make_async_copy(x_hbm, xv, load_sem.at[16])]
    for h in range(2):
        for hh in range(2):
            for c in range(4):
                t = hh * 4 + c
                loads.append(pltpu.make_async_copy(
                    mean_hbm.at[:, :, :, h, hh, :, pl.ds(c * 128, 128)], s_ref.at[h, t], load_sem.at[8 * h + t]))
    for c in loads[1:] + loads[:1]:
        c.start()
    for c in loads[1:]:
        c.wait()
    st[...] = jnp.zeros_like(st)

    @pl.loop(0, 2)
    def _(h):
        for hh in range(2):
            v = [s_ref[h, hh * 4 + c].reshape(512, 128) for c in range(4)]
            sq = (v[0] * v[0] + v[1] * v[1]) + (v[2] * v[2] + v[3] * v[3])
            hrep[h, hh] = jnp.broadcast_to(0.5 * jnp.sum(sq, axis=1, keepdims=True), (512, 128))
        for c in range(4):
            v = cat([s_ref[h, c].reshape(64, 8, 128), s_ref[h, 4 + c].reshape(64, 8, 128)], 1)
            mu[h, c] = v.astype(BF16).reshape(4, 4, 4, 16, 128)

    for i in range(16):
        col = jnp.broadcast_to(lw_ref[i:i + 1, :] * LOG2E, (128, 128)).T
        for g in range(4):
            for r4 in range(4):
                lo = 32 * g + 8 * r4
                lrep[r4 // 2, r4 % 2, (4 * i + g) * 8:(4 * i + g) * 8 + 8, :] = col[lo:lo + 8, :]
    loads[0].wait()

    @pl.loop(0, n_pts // 128)
    def _(i):
        rows = pl.ds(pl.multiple_of(i * 128, 128), 128)
        xb = xv[rows, :].astype(F32)
        sq = xb * xb
        sq = (sq[:, 0:128] + sq[:, 128:256]) + (sq[:, 256:384] + sq[:, 384:512])
        qh[:, rows] = jnp.sum(sq.T, axis=0, keepdims=True) * 0.5

    @pl.loop(0, 2)
    def _(h):
        scores(h, beta_ref[0] * (2.0 * LOG2E))

    bf = (bf_units(0), bf_units(1))

    @pl.loop(0, sweeps - 1)
    def _(sweep):
        b2 = beta_ref[sweep + 1] * (2.0 * LOG2E)
        normalise(lax.rem(sweep, 2))
        moments()
        exchange(bf, update_bf)
        expand(0)

        def next_phase():
            ag_finish(bf[1], 1, 1)
            ag_start(bf[1], 1, 0)

        scores(0, b2, (lambda: ag_relay(bf[1], 1, 1), next_phase, lambda: ag_relay(bf[1], 1, 0)))
        ag_finish(bf[1], 1, 0)
        expand(1)
        scores(1, b2)

    out_lse[...] = normalise((sweeps - 1) % 2) * LN2
    moments()
    f32 = (f32_units(0), f32_units(1))
    exchange(f32, update_f32)
    stores = []
    for h in range(2):
        if h == 1:
            ag_relay(f32[1], 1, 1)
        for hh in range(2):
            for c in range(4):
                t = hh * 4 + c
                stores.append(pltpu.make_async_copy(
                    muf.at[h, t], out_mu.at[:, :, :, h, hh, :, pl.ds(c * 128, 128)], load_sem.at[8 * h + t]))
                if h == 0:
                    stores[-1].start()
    ag_finish(f32[1], 1, 1)
    ag_start(f32[1], 1, 0)
    ag_relay(f32[1], 1, 0)
    ag_finish(f32[1], 1, 0)
    for c in stores[8:]:
        c.start()
    for i in range(16):
        tiles = []
        for g in range(4):
            for r4 in range(4):
                tiles.append(column(muf[r4 // 2, 8, i // 4, i % 4, g], 64 + 32 * (r4 % 2)))
        out_lw[i:i + 1, :] = cat(tiles, 0).T[0:1, :]
    for c in stores:
        c.wait()


def solution(mesh):
    row_groups = mesh.shape["pts"]
    comp_groups = mesh.shape["comp"]

    def per_device(points, mean_vecs, log_w, inv_temp):
        n_pts = points.shape[0]
        n_total = n_pts * row_groups
        k_total = mean_vecs.shape[0] * comp_groups
        sweeps = inv_temp.shape[0]

        def rbuf(k):
            shapes = []
            for (lo, hi), order in zip(SUM_TILES, ORDERS):
                if k == 2:
                    shapes.append(pltpu.VMEM((2, 3, hi - lo, 8, 128), F32))
                    continue
                dims = [2 if d == order[2] else 4 for d in DIMS if d not in order[:k + 1]]
                shapes.append(pltpu.VMEM((2, 6, hi - lo, *dims, 8, 128), F32))
            return shapes

        any_spec = pl.BlockSpec(memory_space=pl.ANY)
        vmem_spec = pl.BlockSpec(memory_space=pltpu.VMEM)
        out_mu, out_lw, out_lse = pl.pallas_call(
            functools.partial(kernel, n_total, k_total, sweeps),
            out_shape=(jax.ShapeDtypeStruct((4, 4, 4, 2, 2, 8, 512), F32),
                       jax.ShapeDtypeStruct((16, 128), F32),
                       jax.ShapeDtypeStruct((1, n_pts), F32)),
            in_specs=[any_spec, any_spec, vmem_spec, pl.BlockSpec(memory_space=pltpu.SMEM)],
            out_specs=(any_spec, vmem_spec, vmem_spec),
            scratch_shapes=[
                pltpu.VMEM((n_pts, 512), BF16),
                pltpu.VMEM((4, 512, n_pts), F32),
                pltpu.VMEM((2, 512, PB), F32),
                pltpu.VMEM((2, 512, PB), F32),
                pltpu.VMEM((2, 9, 4, 4, 4, 8, 128), F32),
                pltpu.VMEM((2, 9, 4, 4, 4, 8, 128), F32),
                pltpu.VMEM((2, 4, 4, 4, 4, 16, 128), BF16),
                pltpu.VMEM((2, 4, 4, 4, 8, 128), F32),
                pltpu.VMEM((2, 2, 512, 128), F32),
                pltpu.VMEM((2, 2, 512, 128), F32),
                pltpu.VMEM((4, 1, n_pts), F32),
                pltpu.VMEM((2, 4, 1, n_pts), F32),
                pltpu.VMEM((2, 1, n_pts), F32),
                pltpu.VMEM((1, n_pts), F32),
                *rbuf(0), *rbuf(1), *rbuf(2),
                pltpu.SemaphoreType.DMA((17,)),
                pltpu.SemaphoreType.DMA,
                pltpu.SemaphoreType.DMA((2,)),
                pltpu.SemaphoreType.DMA((2, 3, 15)),
                pltpu.SemaphoreType.DMA((2, 3, 15)),
                pltpu.SemaphoreType.DMA((2, 4, 15)),
                pltpu.SemaphoreType.DMA((2, 4, 15)),
            ],
            compiler_params=pltpu.CompilerParams(has_side_effects=True, vmem_limit_bytes=67043328),
            cost_estimate=pl.CostEstimate(flops=6 * 2 * n_pts * 2048 * 512, bytes_accessed=1 << 24, transcendentals=0),
        )(points, mean_vecs.reshape(4, 4, 4, 2, 2, 8, 512), log_w.reshape(16, 128), inv_temp)
        return out_mu.reshape(2048, 512), out_lw.reshape(2048), out_lse.reshape(n_pts)

    row_spec = P(("fit", "pts"))
    comp_spec = P(("fit", "comp"))
    return jax.shard_map(
        per_device,
        mesh=mesh,
        in_specs=(P(("fit", "pts"), None), P(("fit", "comp"), None), comp_spec, P()),
        out_specs=(P(("fit", "comp"), None), comp_spec, row_spec),
        check_vma=False,
    )
```

time: 786 us -> 246 us (0.31); the launches traced: 777 us -> 246 us
  blocking collectives: 555 us -> 0 us
  Pallas kernels: 0 us -> 240 us
  matrix products: 110 us -> 0 us
  other arithmetic: 96.3 us -> 0 us
  between operations: 14.1 us -> 0.66 us
    psum x6 -> x0, blocking collectives: 545 us -> none  [the longest x3 534 us: per_device(): counts, stat_sums = lax.psum((counts, stat_sums), 'pts')]
    pallas_call x0 -> x1, Pallas kernels: none -> 240 us  [per_device(): pl.pallas_call(functools.partial(kernel, n_total, k_total, sweeps), out_s...]
    dot_general x6 -> x0, matrix products: 110 us -> none  [the longest x3 57.3 us: per_device(): jnp.einsum('nd,kd->nk', points, mean_bf, preferred_element_type=jnp.float32)]
    reduce_sum x9 -> x0, other arithmetic: 88 us -> none  [the longest x3 39.9 us: per_device(): counts = jnp.sum(resp_prob, axis=0)]
    pmax x3 -> x0, blocking collectives: 10 us -> none  [per_device(): row_top = lax.pmax(jnp.max(logits, axis=1), 'comp')]
  transfers between devices with their start and end apart: 3 -> 0, of which waited for: 0 -> 0; matrix products, arithmetic and copies ran while one was open for 5% -> 0% of each run, Pallas kernels for 0% -> 0%
where the time goes in v2:
time: 246 us
  Pallas kernels  240 us (98%)
  local copies, waits for them, and re-layouts  5.87 us (2%)
    pallas_call x1, Pallas kernels, per_device(): pl.pallas_call(functools.partial(kernel, n_total, k_total, sweeps), out_s...  240 us
    unnamed x7, local copies, waits for them, and re-layouts  5.87 us

profile of v2, /device:TPU:0, one launch (start us, length us, event | category | flops | bytes accessed | tf_op | source)
XLA Modules:
  0.0 246.1 jit_solution(18136781378154074097)
XLA Ops:
  0.6 239.6 %shard_map.67 = (f32[4,4,4,2,2,8,512]{6,5,4,3,2,1,0:T(8,128)}, f32[16,128]{1,0:T(8,128)}, f32[1,4096]{1,0:T(1,128)}) custom-call(bf16[4096,512]{1,0:T(8,128)(2,1)} %x_hbm.1, f32[4,4,4,2,2,8,512]{6,5,4,3,2,1,0:T(8,128)} %bitcast.8, f32[16,128]{1,0:T(8,128)} %bitcast.9, f32[3]{0:T(128)} %beta_ref.1), custom_call_target="tpu_custom_call" | custom-call | flops 51539607552 | bytes 16777216 | tf_op jit(solution)/shard_map/pallas_call | solution.py:414
  240.3 0.0 copy-start.1
  240.3 0.0 copy-start
  240.3 4.7 %copy.10 = f32[2048,512]{1,0:T(8,128)} copy(f32[2048,512]{1,0:T(8,128)} %bitcast.5) | data formatting | bytes 8388608
  244.9 0.0 copy-done.1
  244.9 0.6 copy.11
  245.5 0.0 copy-done
  245.5 0.6 copy.12
Async XLA Ops:
  240.3 4.7 %copy-start.1 = (f32[16,128]{1,0:T(8,128)S(1)}, f32[16,128]{1,0:T(8,128)}, u32[]{:S(2)}) copy-start(f32[16,128]{1,0:T(8,128)} %get-tuple-element.7) | copy-start | bytes 24580
  240.3 5.3 %copy-start = (f32[1,4096]{1,0:T(1,128)S(1)}, f32[1,4096]{1,0:T(1,128)}, u32[]{:S(2)}) copy-start(f32[1,4096]{1,0:T(1,128)} %get-tuple-element.8) | copy-start | bytes 49156

commit v3 on v2

--- a/solution.py
+++ b/solution.py
@@ -296,6 +296,12 @@
         ag_start(u1, 1, 1)
         ag_finish(u0, 0, 0)
 
+    bar = pltpu.get_barrier_semaphore()
+    pl.semaphore_signal(bar, inc=1, device_id=(fit, 1 - comp, pts), device_id_type=MESH)
+    for d in DIMS:
+        for r in (1, 2, 3):
+            pl.semaphore_signal(bar, inc=1, device_id=dev(d, r), device_id_type=MESH)
+
     loads = [pltpu.make_async_copy(x_hbm, xv, load_sem.at[16])]
     for h in range(2):
         for hh in range(2):
@@ -338,6 +344,8 @@
     @pl.loop(0, 2)
     def _(h):
         scores(h, beta_ref[0] * (2.0 * LOG2E))
+
+    pl.semaphore_wait(bar, 10)
 
     bf = (bf_units(0), bf_units(1))
 
@@ -442,7 +450,7 @@
                 pltpu.SemaphoreType.DMA((2, 4, 15)),
                 pltpu.SemaphoreType.DMA((2, 4, 15)),
             ],
-            compiler_params=pltpu.CompilerParams(has_side_effects=True, vmem_limit_bytes=67043328),
+            compiler_params=pltpu.CompilerParams(has_side_effects=True, collective_id=0, vmem_limit_bytes=67043328),
             cost_estimate=pl.CostEstimate(flops=6 * 2 * n_pts * 2048 * 512, bytes_accessed=1 << 24, transcendentals=0),
         )(points, mean_vecs.reshape(4, 4, 4, 2, 2, 8, 512), log_w.reshape(16, 128), inv_temp)
         return out_mu.reshape(2048, 512), out_lw.reshape(2048), out_lse.reshape(n_pts)

time: 246 us -> 238 us (0.967)
  Pallas kernels: 240 us -> 231 us
    pallas_call x1, Pallas kernels: 240 us -> 231 us  [per_device(): pl.pallas_call(functools.partial(kernel, n_total, k_total, sweeps), out_s...]
where the time goes in v3:
time: 238 us; the launch traced here: 237 us
  Pallas kernels  231 us (97%)
  local copies, waits for them, and re-layouts  5.87 us (2%)
    pallas_call x1, Pallas kernels, per_device(): pl.pallas_call(functools.partial(kernel, n_total, k_total, sweeps), out_s...  231 us
    unnamed x7, local copies, waits for them, and re-layouts  5.87 us

profile of v3, /device:TPU:0, one launch (start us, length us, event | category | flops | bytes accessed | tf_op | source)
XLA Modules:
  0.0 237.4 jit_solution(3471940192723410959)
XLA Ops:
  0.6 230.9 %shard_map.67 = (f32[4,4,4,2,2,8,512]{6,5,4,3,2,1,0:T(8,128)}, f32[16,128]{1,0:T(8,128)}, f32[1,4096]{1,0:T(1,128)}) custom-call(bf16[4096,512]{1,0:T(8,128)(2,1)} %x_hbm.1, f32[4,4,4,2,2,8,512]{6,5,4,3,2,1,0:T(8,128)} %bitcast.8, f32[16,128]{1,0:T(8,128)} %bitcast.9, f32[3]{0:T(128)} %beta_ref.1), custom_call_target="tpu_custom_call" | custom-call | flops 51539607552 | bytes 16777216 | tf_op jit(solution)/shard_map/pallas_call | solution.py:422
  231.5 0.0 copy-start.1
  231.5 0.0 copy-start
  231.5 4.7 %copy.10 = f32[2048,512]{1,0:T(8,128)} copy(f32[2048,512]{1,0:T(8,128)} %bitcast.5) | data formatting | bytes 8388608
  236.2 0.0 copy-done.1
  236.2 0.6 copy.11
  236.8 0.0 copy-done
  236.8 0.6 copy.12
Async XLA Ops:
  231.5 4.7 %copy-start.1 = (f32[16,128]{1,0:T(8,128)S(1)}, f32[16,128]{1,0:T(8,128)}, u32[]{:S(2)}) copy-start(f32[16,128]{1,0:T(8,128)} %get-tuple-element.7) | copy-start | bytes 24580
  231.5 5.3 %copy-start = (f32[1,4096]{1,0:T(1,128)S(1)}, f32[1,4096]{1,0:T(1,128)}, u32[]{:S(2)}) copy-start(f32[1,4096]{1,0:T(1,128)} %get-tuple-element.8) | copy-start | bytes 49156

commit v4 on v3

--- a/solution.py
+++ b/solution.py
@@ -267,34 +267,32 @@
         muf[(h, 8) + own] = tile
 
     def exchange(units, upd):
-        u0, u1 = units
         rs_start(1, 0)
         rs_finish(0, 0)
-        rs_start(0, 1)
         rs_relay(1, 0)
-        rs_relay(0, 1)
-        rs_finish(0, 1)
-        rs_start(0, 2)
         rs_finish(1, 0)
-        rs_start(1, 1)
-        rs_finish(0, 2)
-        upd(0)
-        ag_start(u0, 0, 2)
-        rs_relay(1, 1)
-        ag_finish(u0, 0, 2)
-        ag_start(u0, 0, 1)
-        rs_finish(1, 1)
-        rs_start(1, 2)
-        ag_relay(u0, 0, 1)
-        ag_finish(u0, 0, 1)
-        ag_start(u0, 0, 0)
-        rs_finish(1, 2)
-        upd(1)
-        ag_start(u1, 1, 2)
-        ag_relay(u0, 0, 0)
-        ag_finish(u1, 1, 2)
-        ag_start(u1, 1, 1)
-        ag_finish(u0, 0, 0)
+        for k in (1, 2):
+            for h in range(2):
+                rs_start(h, k)
+            if k == 1:
+                for h in range(2):
+                    rs_relay(h, k)
+            for h in range(2):
+                rs_finish(h, k)
+        for h in range(2):
+            upd(h)
+        for k in (2, 1):
+            for h in range(2):
+                ag_start(units[h], h, k)
+            if k == 1:
+                for h in range(2):
+                    ag_relay(units[h], h, k)
+            for h in range(2):
+                ag_finish(units[h], h, k)
+        ag_start(units[0], 0, 0)
+        ag_relay(units[0], 0, 0)
+        ag_start(units[1], 1, 0)
+        ag_finish(units[0], 0, 0)
 
     bar = pltpu.get_barrier_semaphore()
     pl.semaphore_signal(bar, inc=1, device_id=(fit, 1 - comp, pts), device_id_type=MESH)
@@ -357,11 +355,7 @@
         exchange(bf, update_bf)
         expand(0)
 
-        def next_phase():
-            ag_finish(bf[1], 1, 1)
-            ag_start(bf[1], 1, 0)
-
-        scores(0, b2, (lambda: ag_relay(bf[1], 1, 1), next_phase, lambda: ag_relay(bf[1], 1, 0)))
+        scores(0, b2, (lambda: ag_relay(bf[1], 1, 0),))
         ag_finish(bf[1], 1, 0)
         expand(1)
         scores(1, b2)
@@ -373,7 +367,7 @@
     stores = []
     for h in range(2):
         if h == 1:
-            ag_relay(f32[1], 1, 1)
+            ag_relay(f32[1], 1, 0)
         for hh in range(2):
             for c in range(4):
                 t = hh * 4 + c
@@ -381,9 +375,6 @@
                     muf.at[h, t], out_mu.at[:, :, :, h, hh, :, pl.ds(c * 128, 128)], load_sem.at[8 * h + t]))
                 if h == 0:
                     stores[-1].start()
-    ag_finish(f32[1], 1, 1)
-    ag_start(f32[1], 1, 0)
-    ag_relay(f32[1], 1, 0)
     ag_finish(f32[1], 1, 0)
     for c in stores[8:]:
         c.start()

time: 238 us -> 242 us (1.017)
  Pallas kernels: 231 us -> 235 us
    pallas_call x1, Pallas kernels: 231 us -> 235 us  [per_device(): pl.pallas_call(functools.partial(kernel, n_total, k_total, sweeps), out_s...]
where the time goes in v4:
time: 242 us
  Pallas kernels  235 us (97%)
  local copies, waits for them, and re-layouts  5.87 us (2%)
    pallas_call x1, Pallas kernels, per_device(): pl.pallas_call(functools.partial(kernel, n_total, k_total, sweeps), out_s...  235 us
    unnamed x7, local copies, waits for them, and re-layouts  5.87 us

profile of v4, /device:TPU:0, one launch (start us, length us, event | category | flops | bytes accessed | tf_op | source)
XLA Modules:
  0.0 241.5 jit_solution(2644638181935849720)
XLA Ops:
  0.6 235.0 %shard_map.67 = (f32[4,4,4,2,2,8,512]{6,5,4,3,2,1,0:T(8,128)}, f32[16,128]{1,0:T(8,128)}, f32[1,4096]{1,0:T(1,128)}) custom-call(bf16[4096,512]{1,0:T(8,128)(2,1)} %x_hbm.1, f32[4,4,4,2,2,8,512]{6,5,4,3,2,1,0:T(8,128)} %bitcast.8, f32[16,128]{1,0:T(8,128)} %bitcast.9, f32[3]{0:T(128)} %beta_ref.1), custom_call_target="tpu_custom_call" | custom-call | flops 51539607552 | bytes 16777216 | tf_op jit(solution)/shard_map/pallas_call | solution.py:413
  235.6 0.0 copy-start.1
  235.7 0.0 copy-start
  235.7 4.7 %copy.10 = f32[2048,512]{1,0:T(8,128)} copy(f32[2048,512]{1,0:T(8,128)} %bitcast.5) | data formatting | bytes 8388608
  240.3 0.0 copy-done.1
  240.3 0.6 copy.11
  240.9 0.0 copy-done
  240.9 0.6 copy.12
Async XLA Ops:
  235.6 4.7 %copy-start.1 = (f32[16,128]{1,0:T(8,128)S(1)}, f32[16,128]{1,0:T(8,128)}, u32[]{:S(2)}) copy-start(f32[16,128]{1,0:T(8,128)} %get-tuple-element.7) | copy-start | bytes 24580
  235.7 5.3 %copy-start = (f32[1,4096]{1,0:T(1,128)S(1)}, f32[1,4096]{1,0:T(1,128)}, u32[]{:S(2)}) copy-start(f32[1,4096]{1,0:T(1,128)} %get-tuple-element.8) | copy-start | bytes 49156

commit v5 on v3

--- a/solution.py
+++ b/solution.py
@@ -27,8 +27,8 @@
     return jnp.concatenate(parts, axis=axis)
 
 
-def kernel(n_total, k_total, sweeps, x_hbm, mean_hbm, lw_ref, beta_ref, out_mu, out_lw, out_lse,
-           xv, e_ref, l0, l1, s_ref, muf, mu, ct, hrep, lrep, st, stp, wrow, qh,
+def kernel(n_total, k_total, sweeps, x_hbm, mean_hbm, lw_ref, beta_ref, muf, out_lse,
+           xv, e_ref, l0, l1, s_ref, mu, ct, hrep, lrep, st, stp, wrow, qh,
            ra0, ra1, ra2, rb0, rb1, rb2, rc0, rc1, rc2,
            load_sem, ex_send, ex_recv, rs_send, rs_recv, ag_send, ag_recv):
     n_pts = xv.shape[0]
@@ -77,8 +77,8 @@
         j = 6 * k + i
         return remote(src, buf.at[h, i], rs_send.at[h, p, j], rs_recv.at[h, p, j], dev(d, r))
 
-    def rs_start(h, k):
-        for i in ((2, 0, 1) if k == 2 else (0, 1, 3, 4)):
+    def rs_start(h, k, which=(0, 1, 3, 4)):
+        for i in ((2, 0, 1) if k == 2 else which):
             for p in range(3):
                 rs_copy(h, p, k, i).start()
 
@@ -268,11 +268,12 @@
 
     def exchange(units, upd):
         u0, u1 = units
-        rs_start(1, 0)
+        rs_start(1, 0, (0, 1))
         rs_finish(0, 0)
         rs_start(0, 1)
+        rs_start(1, 0, (3, 4))
+        rs_relay(0, 1)
         rs_relay(1, 0)
-        rs_relay(0, 1)
         rs_finish(0, 1)
         rs_start(0, 2)
         rs_finish(1, 0)
@@ -333,7 +334,7 @@
                 lrep[r4 // 2, r4 % 2, (4 * i + g) * 8:(4 * i + g) * 8 + 8, :] = col[lo:lo + 8, :]
     loads[0].wait()
 
-    @pl.loop(0, n_pts // 128)
+    @pl.loop(0, n_pts // 128, unroll=4)
     def _(i):
         rows = pl.ds(pl.multiple_of(i * 128, 128), 128)
         xb = xv[rows, :].astype(F32)
@@ -370,29 +371,31 @@
     moments()
     f32 = (f32_units(0), f32_units(1))
     exchange(f32, update_f32)
-    stores = []
-    for h in range(2):
-        if h == 1:
-            ag_relay(f32[1], 1, 1)
-        for hh in range(2):
-            for c in range(4):
-                t = hh * 4 + c
-                stores.append(pltpu.make_async_copy(
-                    muf.at[h, t], out_mu.at[:, :, :, h, hh, :, pl.ds(c * 128, 128)], load_sem.at[8 * h + t]))
-                if h == 0:
-                    stores[-1].start()
+    ag_relay(f32[1], 1, 1)
     ag_finish(f32[1], 1, 1)
     ag_start(f32[1], 1, 0)
     ag_relay(f32[1], 1, 0)
     ag_finish(f32[1], 1, 0)
-    for c in stores[8:]:
-        c.start()
+
+
+def write_out(muf, lse, out_mu, out_lw, out_lse, sem):
+    stores = []
+    for h in range(2):
+        for hh in range(2):
+            for c in range(4):
+                t = hh * 4 + c
+                stores.append(pltpu.make_async_copy(
+                    muf.at[h, t], out_mu.at[:, :, :, h, hh, :, pl.ds(c * 128, 128)], sem.at[8 * h + t]))
+                stores[-1].start()
     for i in range(16):
         tiles = []
         for g in range(4):
             for r4 in range(4):
-                tiles.append(column(muf[r4 // 2, 8, i // 4, i % 4, g], 64 + 32 * (r4 % 2)))
+                v = muf[r4 // 2, 8, i // 4, i % 4, g]
+                lo = 64 + 32 * (r4 % 2)
+                tiles.append(jnp.broadcast_to(v[:, lo:lo + 1], (8, 128)))
         out_lw[i:i + 1, :] = cat(tiles, 0).T[0:1, :]
+    out_lse[...] = lse[...]
     for c in stores:
         c.wait()
 
@@ -419,19 +422,16 @@
 
         any_spec = pl.BlockSpec(memory_space=pl.ANY)
         vmem_spec = pl.BlockSpec(memory_space=pltpu.VMEM)
-        out_mu, out_lw, out_lse = pl.pallas_call(
+        muf, lse = pl.pallas_call(
             functools.partial(kernel, n_total, k_total, sweeps),
-            out_shape=(jax.ShapeDtypeStruct((4, 4, 4, 2, 2, 8, 512), F32),
-                       jax.ShapeDtypeStruct((16, 128), F32),
-                       jax.ShapeDtypeStruct((1, n_pts), F32)),
+            out_shape=(pltpu.VMEM((2, 9, 4, 4, 4, 8, 128), F32), pltpu.VMEM((1, n_pts), F32)),
             in_specs=[any_spec, any_spec, vmem_spec, pl.BlockSpec(memory_space=pltpu.SMEM)],
-            out_specs=(any_spec, vmem_spec, vmem_spec),
+            out_specs=(vmem_spec, vmem_spec),
             scratch_shapes=[
                 pltpu.VMEM((n_pts, 512), BF16),
                 pltpu.VMEM((4, 512, n_pts), F32),
                 pltpu.VMEM((2, 512, PB), F32),
                 pltpu.VMEM((2, 512, PB), F32),
-                pltpu.VMEM((2, 9, 4, 4, 4, 8, 128), F32),
                 pltpu.VMEM((2, 9, 4, 4, 4, 8, 128), F32),
                 pltpu.VMEM((2, 4, 4, 4, 4, 16, 128), BF16),
                 pltpu.VMEM((2, 4, 4, 4, 8, 128), F32),
@@ -450,9 +450,19 @@
                 pltpu.SemaphoreType.DMA((2, 4, 15)),
                 pltpu.SemaphoreType.DMA((2, 4, 15)),
             ],
-            compiler_params=pltpu.CompilerParams(has_side_effects=True, collective_id=0, vmem_limit_bytes=67043328),
+            compiler_params=pltpu.CompilerParams(has_side_effects=True, collective_id=0, vmem_limit_bytes=61000000),
             cost_estimate=pl.CostEstimate(flops=6 * 2 * n_pts * 2048 * 512, bytes_accessed=1 << 24, transcendentals=0),
         )(points, mean_vecs.reshape(4, 4, 4, 2, 2, 8, 512), log_w.reshape(16, 128), inv_temp)
+        out_mu, out_lw, out_lse = pl.pallas_call(
+            write_out,
+            out_shape=(jax.ShapeDtypeStruct((4, 4, 4, 2, 2, 8, 512), F32),
+                       jax.ShapeDtypeStruct((16, 128), F32),
+                       jax.ShapeDtypeStruct((1, n_pts), F32)),
+            in_specs=[vmem_spec, vmem_spec],
+            out_specs=(any_spec, vmem_spec, vmem_spec),
+            scratch_shapes=[pltpu.SemaphoreType.DMA((16,))],
+            compiler_params=pltpu.CompilerParams(vmem_limit_bytes=16 << 20),
+        )(muf, lse)
         return out_mu.reshape(2048, 512), out_lw.reshape(2048), out_lse.reshape(n_pts)
 
     row_spec = P(("fit", "pts"))

time: 238 us -> 222 us (0.933)
  Pallas kernels: 231 us -> 221 us
  local copies, waits for them, and re-layouts: 5.87 us -> 0 us
    pallas_call x1, Pallas kernels: 231 us -> 218 us  [per_device(): pl.pallas_call(functools.partial(kernel, n_total, k_total, sweeps), out_s...]
    unnamed x7 -> x0, local copies, waits for them, and re-layouts: 5.87 us -> none
    pallas_call x0 -> x1, Pallas kernels: none -> 2.76 us  [per_device(): pl.pallas_call(write_out, out_shape=(jax.ShapeDtypeStruct((4, 4, 4, 2, 2,...]
where the time goes in v5:
time: 222 us
  Pallas kernels  221 us (100%)
    pallas_call x1, Pallas kernels, per_device(): pl.pallas_call(functools.partial(kernel, n_total, k_total, sweeps), out_s...  218 us

profile of v5, /device:TPU:0, one launch (start us, length us, event | category | flops | bytes accessed | tf_op | source)
XLA Modules:
  0.0 221.6 jit_solution(13427009669678173929)
XLA Ops:
  0.6 218.0 %shard_map.67 = (f32[2,9,4,4,4,8,128]{6,5,4,3,2,1,0:T(8,128)S(1)}, f32[1,4096]{1,0:T(1,128)S(1)}) custom-call(bf16[4096,512]{1,0:T(8,128)(2,1)} %x_hbm.1, f32[4,4,4,2,2,8,512]{6,5,4,3,2,1,0:T(8,128)} %bitcast.5, f32[16,128]{1,0:T(8,128)} %bitcast.8, f32[3]{0:T(128)} %beta_ref.1), custom_call_target="tpu_custom_call" | custom-call | flops 51539607552 | bytes 16777216 | tf_op jit(solution)/shard_map/pallas_call | solution.py:425
  218.6 2.8 %shard_map.68 = (f32[4,4,4,2,2,8,512]{6,5,4,3,2,1,0:T(8,128)}, f32[16,128]{1,0:T(8,128)}, f32[1,4096]{1,0:T(1,128)}) custom-call(f32[2,9,4,4,4,8,128]{6,5,4,3,2,1,0:T(8,128)S(1)} %get-tuple-element.8.muf, f32[1,4096]{1,0:T(1,128)S(1)} %get-tuple-element.9.lse), custom_call_target="tpu_custom_call" | custom-call | tf_op jit(solution)/shard_map/pallas_call | solution.py:456

commit v6 on v5

--- a/solution.py
+++ b/solution.py
@@ -194,10 +194,10 @@
         def _(i):
             for n, step in enumerate(during):
                 pl.when(i == n)(step)
+            exps(h, 2 * i, l0)
             logits(h, 2 * i + 1, l1, b2)
-            exps(h, 2 * i, l0)
+            exps(h, 2 * i + 1, l1)
             logits(h, 2 * i + 2, l0, b2)
-            exps(h, 2 * i + 1, l1)
 
         logits(h, nb - 1, l1, b2)
         exps(h, nb - 2, l0)
@@ -276,17 +276,17 @@
         rs_relay(1, 0)
         rs_finish(0, 1)
         rs_start(0, 2)
-        rs_finish(1, 0)
-        rs_start(1, 1)
         rs_finish(0, 2)
         upd(0)
         ag_start(u0, 0, 2)
-        rs_relay(1, 1)
+        rs_finish(1, 0)
+        rs_start(1, 1)
         ag_finish(u0, 0, 2)
         ag_start(u0, 0, 1)
+        rs_relay(1, 1)
+        ag_relay(u0, 0, 1)
         rs_finish(1, 1)
         rs_start(1, 2)
-        ag_relay(u0, 0, 1)
         ag_finish(u0, 0, 1)
         ag_start(u0, 0, 0)
         rs_finish(1, 2)
@@ -310,22 +310,9 @@
                 t = hh * 4 + c
                 loads.append(pltpu.make_async_copy(
                     mean_hbm.at[:, :, :, h, hh, :, pl.ds(c * 128, 128)], s_ref.at[h, t], load_sem.at[8 * h + t]))
-    for c in loads[1:] + loads[:1]:
+    for c in loads[1:9] + loads[:1] + loads[9:]:
         c.start()
-    for c in loads[1:]:
-        c.wait()
     st[...] = jnp.zeros_like(st)
-
-    @pl.loop(0, 2)
-    def _(h):
-        for hh in range(2):
-            v = [s_ref[h, hh * 4 + c].reshape(512, 128) for c in range(4)]
-            sq = (v[0] * v[0] + v[1] * v[1]) + (v[2] * v[2] + v[3] * v[3])
-            hrep[h, hh] = jnp.broadcast_to(0.5 * jnp.sum(sq, axis=1, keepdims=True), (512, 128))
-        for c in range(4):
-            v = cat([s_ref[h, c].reshape(64, 8, 128), s_ref[h, 4 + c].reshape(64, 8, 128)], 1)
-            mu[h, c] = v.astype(BF16).reshape(4, 4, 4, 16, 128)
-
     for i in range(16):
         col = jnp.broadcast_to(lw_ref[i:i + 1, :] * LOG2E, (128, 128)).T
         for g in range(4):
@@ -342,8 +329,18 @@
         sq = (sq[:, 0:128] + sq[:, 128:256]) + (sq[:, 256:384] + sq[:, 384:512])
         qh[:, rows] = jnp.sum(sq.T, axis=0, keepdims=True) * 0.5
 
+    for c in loads[1:]:
+        c.wait()
+
     @pl.loop(0, 2)
     def _(h):
+        for hh in range(2):
+            v = [s_ref[h, hh * 4 + c].reshape(512, 128) for c in range(4)]
+            sq = (v[0] * v[0] + v[1] * v[1]) + (v[2] * v[2] + v[3] * v[3])
+            hrep[h, hh] = jnp.broadcast_to(0.5 * jnp.sum(sq, axis=1, keepdims=True), (512, 128))
+        for c in range(4):
+            v = cat([s_ref[h, c].reshape(64, 8, 128), s_ref[h, 4 + c].reshape(64, 8, 128)], 1)
+            mu[h, c] = v.astype(BF16).reshape(4, 4, 4, 16, 128)
         scores(h, beta_ref[0] * (2.0 * LOG2E))
 
     pl.semaphore_wait(bar, 10)

time: 222 us -> 221 us (level)
  no operation moved by 1% of the time
where the time goes in v6:
time: 221 us
  Pallas kernels  220 us (100%)
    pallas_call x1, Pallas kernels, per_device(): pl.pallas_call(functools.partial(kernel, n_total, k_total, sweeps), out_s...  218 us

profile of v6, /device:TPU:0, one launch (start us, length us, event | category | flops | bytes accessed | tf_op | source)
XLA Modules:
  0.0 221.2 jit_solution(12081920270900871799)
XLA Ops:
  0.6 217.6 %shard_map.67 = (f32[2,9,4,4,4,8,128]{6,5,4,3,2,1,0:T(8,128)S(1)}, f32[1,4096]{1,0:T(1,128)S(1)}) custom-call(bf16[4096,512]{1,0:T(8,128)(2,1)} %x_hbm.1, f32[4,4,4,2,2,8,512]{6,5,4,3,2,1,0:T(8,128)} %bitcast.5, f32[16,128]{1,0:T(8,128)} %bitcast.8, f32[3]{0:T(128)} %beta_ref.1), custom_call_target="tpu_custom_call" | custom-call | flops 51539607552 | bytes 16777216 | tf_op jit(solution)/shard_map/pallas_call | solution.py:422
  218.2 2.8 %shard_map.68 = (f32[4,4,4,2,2,8,512]{6,5,4,3,2,1,0:T(8,128)}, f32[16,128]{1,0:T(8,128)}, f32[1,4096]{1,0:T(1,128)}) custom-call(f32[2,9,4,4,4,8,128]{6,5,4,3,2,1,0:T(8,128)S(1)} %get-tuple-element.8.muf, f32[1,4096]{1,0:T(1,128)S(1)} %get-tuple-element.9.lse), custom_call_target="tpu_custom_call" | custom-call | tf_op jit(solution)/shard_map/pallas_call | solution.py:453

commit v7 on v6

--- a/solution.py
+++ b/solution.py
@@ -64,7 +64,7 @@
 
     def rs_copy(h, p, k, i):
         d, buf = ORDERS[p][k], bufs[k][p]
-        if k == 2:
+        if k >= 1:
             r = (1, 3, 2)[i]
             src = s_ref.at[sums(h, p) + place(p, k, r)]
         else:
@@ -78,7 +78,7 @@
         return remote(src, buf.at[h, i], rs_send.at[h, p, j], rs_recv.at[h, p, j], dev(d, r))
 
     def rs_start(h, k, which=(0, 1, 3, 4)):
-        for i in ((2, 0, 1) if k == 2 else which):
+        for i in ((2, 0, 1) if k >= 1 else which):
             for p in range(3):
                 rs_copy(h, p, k, i).start()
 
@@ -93,10 +93,10 @@
     def rs_finish(h, k):
         for p in range(3):
             buf = bufs[k][p]
-            if k == 2:
+            if k >= 1:
                 for i in range(3):
                     rs_copy(h, p, k, i).wait()
-                mine = sums(h, p) + own
+                mine = sums(h, p) + place(p, k, 0)
                 s_ref[mine] = (s_ref[mine] + buf[h, 0]) + (buf[h, 1] + buf[h, 2])
                 continue
             for half, i, j in ((0, 2, 4), (1, 3, 5)):
@@ -119,7 +119,7 @@
     def ag_copy(units, h, u, k, i):
         ref, lead, p = units[u]
         d = ORDERS[p][k]
-        if k == 2:
+        if k >= 1:
             r = (1, 3, 2)[i]
             view = ref.at[lead + place(p, k, 0)]
         else:
@@ -129,7 +129,7 @@
         return remote(view, view, ag_send.at[h, u, j], ag_recv.at[h, u, j], dev(d, r))
 
     def ag_start(units, h, k):
-        for i in ((2, 0, 1) if k == 2 else range(4)):
+        for i in ((2, 0, 1) if k >= 1 else range(4)):
             for u in range(len(units)):
                 ag_copy(units, h, u, k, i).start()
 
@@ -141,7 +141,7 @@
 
     def ag_finish(units, h, k):
         for u in range(len(units)):
-            if k == 2:
+            if k >= 1:
                 for i in range(3):
                     ag_copy(units, h, u, k, i).wait()
                 continue
@@ -192,7 +192,7 @@
 
         @pl.loop(0, nb // 2 - 1)
         def _(i):
-            for n, step in enumerate(during):
+            for n, step in during:
                 pl.when(i == n)(step)
             exps(h, 2 * i, l0)
             logits(h, 2 * i + 1, l1, b2)
@@ -272,7 +272,6 @@
         rs_finish(0, 0)
         rs_start(0, 1)
         rs_start(1, 0, (3, 4))
-        rs_relay(0, 1)
         rs_relay(1, 0)
         rs_finish(0, 1)
         rs_start(0, 2)
@@ -283,8 +282,6 @@
         rs_start(1, 1)
         ag_finish(u0, 0, 2)
         ag_start(u0, 0, 1)
-        rs_relay(1, 1)
-        ag_relay(u0, 0, 1)
         rs_finish(1, 1)
         rs_start(1, 2)
         ag_finish(u0, 0, 1)
@@ -359,7 +356,7 @@
             ag_finish(bf[1], 1, 1)
             ag_start(bf[1], 1, 0)
 
-        scores(0, b2, (lambda: ag_relay(bf[1], 1, 1), next_phase, lambda: ag_relay(bf[1], 1, 0)))
+        scores(0, b2, ((0, next_phase), (2, lambda: ag_relay(bf[1], 1, 0))))
         ag_finish(bf[1], 1, 0)
         expand(1)
         scores(1, b2)
@@ -368,7 +365,6 @@
     moments()
     f32 = (f32_units(0), f32_units(1))
     exchange(f32, update_f32)
-    ag_relay(f32[1], 1, 1)
     ag_finish(f32[1], 1, 1)
     ag_start(f32[1], 1, 0)
     ag_relay(f32[1], 1, 0)
@@ -410,8 +406,8 @@
         def rbuf(k):
             shapes = []
             for (lo, hi), order in zip(SUM_TILES, ORDERS):
-                if k == 2:
-                    shapes.append(pltpu.VMEM((2, 3, hi - lo, 8, 128), F32))
+                if k >= 1:
+                    shapes.append(pltpu.VMEM((2, 3, hi - lo, *((4,) * (2 - k)), 8, 128), F32))
                     continue
                 dims = [2 if d == order[2] else 4 for d in DIMS if d not in order[:k + 1]]
                 shapes.append(pltpu.VMEM((2, 6, hi - lo, *dims, 8, 128), F32))

time: 221 us -> 204 us (0.923)
  Pallas kernels: 220 us -> 203 us
    pallas_call x1, Pallas kernels: 218 us -> 200 us  [per_device(): pl.pallas_call(functools.partial(kernel, n_total, k_total, sweeps), out_s...]
where the time goes in v7:
time: 204 us
  Pallas kernels  203 us (100%)
    pallas_call x1, Pallas kernels, per_device(): pl.pallas_call(functools.partial(kernel, n_total, k_total, sweeps), out_s...  200 us

profile of v7, /device:TPU:0, one launch (start us, length us, event | category | flops | bytes accessed | tf_op | source)
XLA Modules:
  0.0 203.6 jit_solution(14382721636196088341)
XLA Ops:
  0.6 200.0 %shard_map.67 = (f32[2,9,4,4,4,8,128]{6,5,4,3,2,1,0:T(8,128)S(1)}, f32[1,4096]{1,0:T(1,128)S(1)}) custom-call(bf16[4096,512]{1,0:T(8,128)(2,1)} %x_hbm.1, f32[4,4,4,2,2,8,512]{6,5,4,3,2,1,0:T(8,128)} %bitcast.5, f32[16,128]{1,0:T(8,128)} %bitcast.8, f32[3]{0:T(128)} %beta_ref.1), custom_call_target="tpu_custom_call" | custom-call | flops 51539607552 | bytes 16777216 | tf_op jit(solution)/shard_map/pallas_call | solution.py:418
  200.6 2.8 %shard_map.68 = (f32[4,4,4,2,2,8,512]{6,5,4,3,2,1,0:T(8,128)}, f32[16,128]{1,0:T(8,128)}, f32[1,4096]{1,0:T(1,128)}) custom-call(f32[2,9,4,4,4,8,128]{6,5,4,3,2,1,0:T(8,128)S(1)} %get-tuple-element.8.muf, f32[1,4096]{1,0:T(1,128)S(1)} %get-tuple-element.9.lse), custom_call_target="tpu_custom_call" | custom-call | tf_op jit(solution)/shard_map/pallas_call | solution.py:449

commit v8 on v7

--- a/solution.py
+++ b/solution.py
@@ -116,10 +116,13 @@
     def f32_units(h):
         return [(muf, sums(h, p), p) for p in range(3)]
 
+    def straight(units, k):
+        return k >= 1 or units[0][0] is mu
+
     def ag_copy(units, h, u, k, i):
         ref, lead, p = units[u]
         d = ORDERS[p][k]
-        if k >= 1:
+        if straight(units, k):
             r = (1, 3, 2)[i]
             view = ref.at[lead + place(p, k, 0)]
         else:
@@ -129,11 +132,13 @@
         return remote(view, view, ag_send.at[h, u, j], ag_recv.at[h, u, j], dev(d, r))
 
     def ag_start(units, h, k):
-        for i in ((2, 0, 1) if k >= 1 else range(4)):
+        for i in ((2, 0, 1) if straight(units, k) else range(4)):
             for u in range(len(units)):
                 ag_copy(units, h, u, k, i).start()
 
     def ag_relay(units, h, k):
+        if straight(units, k):
+            return
         for u in range(len(units)):
             for i, nxt in ((0, 4), (1, 5)):
                 ag_copy(units, h, u, k, i).wait_recv()
@@ -141,7 +146,7 @@
 
     def ag_finish(units, h, k):
         for u in range(len(units)):
-            if k >= 1:
+            if straight(units, k):
                 for i in range(3):
                     ag_copy(units, h, u, k, i).wait()
                 continue
@@ -356,7 +361,7 @@
             ag_finish(bf[1], 1, 1)
             ag_start(bf[1], 1, 0)
 
-        scores(0, b2, ((0, next_phase), (2, lambda: ag_relay(bf[1], 1, 0))))
+        scores(0, b2, ((0, next_phase),))
         ag_finish(bf[1], 1, 0)
         expand(1)
         scores(1, b2)

time: 204 us -> 206 us (level)
    pallas_call x1, Pallas kernels: 200 us -> 203 us  [per_device(): pl.pallas_call(functools.partial(kernel, n_total, k_total, sweeps), out_s...]
where the time goes in v8:
time: 206 us
  Pallas kernels  205 us (100%)
    pallas_call x1, Pallas kernels, per_device(): pl.pallas_call(functools.partial(kernel, n_total, k_total, sweeps), out_s...  203 us

profile of v8, /device:TPU:0, one launch (start us, length us, event | category | flops | bytes accessed | tf_op | source)
XLA Modules:
  0.0 206.3 jit_solution(13785693917108922970)
XLA Ops:
  0.6 202.7 %shard_map.67 = (f32[2,9,4,4,4,8,128]{6,5,4,3,2,1,0:T(8,128)S(1)}, f32[1,4096]{1,0:T(1,128)S(1)}) custom-call(bf16[4096,512]{1,0:T(8,128)(2,1)} %x_hbm.1, f32[4,4,4,2,2,8,512]{6,5,4,3,2,1,0:T(8,128)} %bitcast.5, f32[16,128]{1,0:T(8,128)} %bitcast.8, f32[3]{0:T(128)} %beta_ref.1), custom_call_target="tpu_custom_call" | custom-call | flops 51539607552 | bytes 16777216 | tf_op jit(solution)/shard_map/pallas_call | solution.py:423
  203.3 2.8 %shard_map.68 = (f32[4,4,4,2,2,8,512]{6,5,4,3,2,1,0:T(8,128)}, f32[16,128]{1,0:T(8,128)}, f32[1,4096]{1,0:T(1,128)}) custom-call(f32[2,9,4,4,4,8,128]{6,5,4,3,2,1,0:T(8,128)S(1)} %get-tuple-element.8.muf, f32[1,4096]{1,0:T(1,128)S(1)} %get-tuple-element.9.lse), custom_call_target="tpu_custom_call" | custom-call | tf_op jit(solution)/shard_map/pallas_call | solution.py:454
